TPU v7x, 32 devices: a whole 2x2x4 slice. The times are simulated.
32 devices in a mesh: space: 16 (over z, y, core), tm: 2 (over x).
Axes of the slice: x: 2, y: 2, z: 4, core: 2. Of those that a mesh axis runs over, the one named last changes fastest.
Arguments:
- solutions: bfloat16 [2, 12, 8192, 128], P('tm', None, 'space'), may hold values from -6 to 6
- noise: int32 [2, 64, 12, 8192], P('tm', None, None, 'space'), may hold values from 0 to 3
- momenta: int32 [27, 3], replicated, may hold values from -2 to 2
- pairs: int32 [16, 2], P('tm'), may hold values from 0 to 1
Outputs:
- mesons: float32 [2, 2, 27, 64, 64], P('tm', None, None, 'space')
- correlators: float32 [16, 2, 27], P('tm')
All inputs are finite; a program needn't handle non-finite values.
Results may differ from a plain program's by a relative error of at most 0.002.
Values sent between devices are 32-bit elements; how exact they have to be, the bound alone decides.
A program may use at most 64 MiB of HBM per device.

v0:
```python
import math
import jax
import jax.numpy as jnp
from jax import lax
from jax.sharding import PartitionSpec as P

EXTENT = 48


def phase_weights(noise_block, momenta, coords):
    qdotx = (
        momenta[:, 0:1] * coords[0][None, :]
        + momenta[:, 1:2] * coords[1][None, :]
        + momenta[:, 2:3] * coords[2][None, :]
    )
    base_index = qdotx % EXTENT
    angle = base_index.astype(jnp.float32) * jnp.float32(2.0 * math.pi / EXTENT)
    base_re = jnp.cos(angle).astype(jnp.bfloat16)[:, None, None, :]
    base_im = (-jnp.sin(angle)).astype(jnp.bfloat16)[:, None, None, :]
    turns = (noise_block % 4)[None, :, :, :]
    weight_re = jnp.where(
        turns == 0,
        base_re,
        jnp.where(turns == 1, base_im, jnp.where(turns == 2, -base_re, -base_im)),
    )
    weight_im = jnp.where(
        turns == 0,
        base_im,
        jnp.where(turns == 1, -base_re, jnp.where(turns == 2, -base_im, base_re)),
    )
    rows = momenta.shape[0] * noise_block.shape[0]
    cols = noise_block.shape[1] * noise_block.shape[2]
    return (weight_re.reshape(rows, cols), weight_im.reshape(rows, cols))


def partial_field(vectors, sources, momenta, offset):
    spincol, sites, width = vectors.shape
    nvec = width // 2
    moms = momenta.shape[0]
    block = min(128, sites)
    nblocks = sites // block

    def one_block(step, total):
        first = (step * block).astype(jnp.int32)
        noise_block = lax.dynamic_slice_in_dim(sources, first, block, 2)
        vec_block = lax.dynamic_slice_in_dim(vectors, first, block, 1)
        glob = offset + first + jnp.arange(block, dtype=jnp.int32)
        coords = (glob % EXTENT, glob // EXTENT % EXTENT, glob // (EXTENT * EXTENT))
        weight_re, weight_im = phase_weights(noise_block, momenta, coords)
        stacked = vec_block.reshape(spincol * block, width)
        left = jnp.dot(weight_re, stacked, preferred_element_type=jnp.float32)
        right = jnp.dot(weight_im, stacked, preferred_element_type=jnp.float32)
        real_part = left[:, :nvec] - right[:, nvec:]
        imag_part = left[:, nvec:] + right[:, :nvec]
        return total + jnp.stack([real_part, imag_part], 0)

    start = jnp.zeros((2, moms * nvec, nvec), jnp.float32)
    total = lax.fori_loop(0, nblocks, one_block, start)
    return total.reshape(2, moms, nvec, nvec)


def pair_traces(fields, pairs):
    nslices = fields.shape[0]
    slots = jnp.arange(nslices, dtype=jnp.int32)
    pick_sink = (pairs[:, 1][:, None] == slots[None, :]).astype(jnp.float32)
    pick_source = (pairs[:, 0][:, None] == slots[None, :]).astype(jnp.float32)
    sink = jnp.einsum("kt,tcpij->kcpij", pick_sink, fields, precision=lax.Precision.HIGHEST)
    source = jnp.einsum("kt,tcpij->kcpij", pick_source, fields, precision=lax.Precision.HIGHEST)
    real_part = jnp.sum(sink[:, 0] * source[:, 0] + sink[:, 1] * source[:, 1], axis=(2, 3))
    imag_part = jnp.sum(sink[:, 1] * source[:, 0] - sink[:, 0] * source[:, 1], axis=(2, 3))
    return jnp.stack([real_part, imag_part], 1)


def local(solutions, noise, momenta, pairs):
    slice_count, spincol, sites_local, width = solutions.shape
    nvec = width // 2
    nspace = lax.axis_size("space")
    scale = 1.0 / math.sqrt(spincol * sites_local * nspace)
    offset = lax.axis_index("space") * sites_local
    terms = jnp.stack([partial_field(solutions[0], noise[0], momenta, offset) * scale], 0)
    mesons = lax.psum_scatter(terms, "space", scatter_dimension=3, tiled=True)
    every_slice = lax.all_gather(mesons, "tm", axis=0, tiled=True)
    partial_traces = pair_traces(every_slice, pairs)
    correlators = lax.psum(partial_traces, "space") / nvec
    return (mesons, correlators)


def solution(mesh):
    in_specs = (P("tm", None, "space", None), P("tm", None, None, "space"), P(), P("tm", None))
    out_specs = (P("tm", None, None, "space", None), P("tm", None, None))
    return jax.shard_map(local, mesh=mesh, in_specs=in_specs, out_specs=out_specs, check_vma=False)
```

profile of v0, /device:TPU:0, one launch (start us, length us, event | category | flops | bytes accessed | tf_op | source)
XLA Modules:
  0.0 223.5 jit_solution(1606789766485243148)
XLA Ops:
  7.2 3.7 %copy.53 = s32[1,64,12,512]{3,2,1,0:T(8,128)} copy(s32[1,64,12,512]{3,1,2,0:T(8,128)} %param.7) | data formatting | bytes 3145728 | tf_op args[1]
  11.0 64.5 %while.17 = (s32[]{:T(128)}, f32[2,1728,64]{2,1,0:T(8,128)S(1)}, s32[64,12,512]{2,1,0:T(8,128)}, s32[27,3]{0,1:T(4,128)S(1)}, s32[]{:T(128)}, /*index=5*/bf16[12...) while((s32[]{:T(128)}, f32[2,1728,64]{2,1,0:T(8,128)S(1)}, ...), condition=%wide.region_1.2_spmd.clone, body=%wide.region_0.1_spmd.clone.sunk | while | flops 1377275648 | bytes 30928840 | solution.py:58
  11.4 1.4 broadcast_compare_fusion.4
  12.8 6.0 %select_select_fusion.3 = (bf16[27,64,12,128]{3,2,1,0:T(8,128)(2,1)}, bf16[27,64,12,128]{3,2,1,0:T(8,128)(2,1)S(1)}) fusion(pred[64,12,128]{2,1,0:T(8,128)(4,1)S(1)} %get-tuple-element.309, pred[64,12,128]{2,1,0:T(8,128)(4,1)S(1)} %get-tuple-element.310, pred[64,12,128]{2,1,0:T(8,128)(4,1)S(1)} %get-tuple-element.311, ...), kind=kLoop, calls=%fused_computation.1.clone.1 | loop fusion | flops 15925248 | bytes 10939392 | tf_op jit(solution)/shard_map/while/body/eval_jaxpr/jit(_where)/select_n | solution.py:21
  18.8 1.0 constant_dynamic-slice_fusion.3
  19.8 4.6 %fusion.46 = f32[1728,128]{1,0:T(8,128)S(1)} fusion(bf16[1536,128]{1,0:T(8,128)(2,1)S(1)} %bitcast.66, bf16[216,8,12,128]{3,2,1,0:T(8,128)(2,1)} %bitcast.64), kind=kOutput, calls=%fused_computation.5.clone.1 | convolution fusion | flops 679477248 | bytes 6586368 | tf_op jit(solution)/shard_map/while/body/eval_jaxpr/dot_general | solution.py:51
  24.4 1.6 fusion.45
  27.5 1.4 broadcast_compare_fusion.4
  29.0 6.0 %select_select_fusion.3 = (bf16[27,64,12,128]{3,2,1,0:T(8,128)(2,1)}, bf16[27,64,12,128]{3,2,1,0:T(8,128)(2,1)S(1)}) fusion(pred[64,12,128]{2,1,0:T(8,128)(4,1)S(1)} %get-tuple-element.309, pred[64,12,128]{2,1,0:T(8,128)(4,1)S(1)} %get-tuple-element.310, pred[64,12,128]{2,1,0:T(8,128)(4,1)S(1)} %get-tuple-element.311, ...), kind=kLoop, calls=%fused_computation.1.clone.1 | loop fusion | flops 15925248 | bytes 10939392 | tf_op jit(solution)/shard_map/while/body/eval_jaxpr/jit(_where)/select_n | solution.py:21
  35.9 4.6 %fusion.46 = f32[1728,128]{1,0:T(8,128)S(1)} fusion(bf16[1536,128]{1,0:T(8,128)(2,1)S(1)} %bitcast.66, bf16[216,8,12,128]{3,2,1,0:T(8,128)(2,1)} %bitcast.64), kind=kOutput, calls=%fused_computation.5.clone.1 | convolution fusion | flops 679477248 | bytes 6586368 | tf_op jit(solution)/shard_map/while/body/eval_jaxpr/dot_general | solution.py:51
  40.5 1.6 fusion.45
  43.6 1.4 broadcast_compare_fusion.4
  45.1 6.0 %select_select_fusion.3 = (bf16[27,64,12,128]{3,2,1,0:T(8,128)(2,1)}, bf16[27,64,12,128]{3,2,1,0:T(8,128)(2,1)S(1)}) fusion(pred[64,12,128]{2,1,0:T(8,128)(4,1)S(1)} %get-tuple-element.309, pred[64,12,128]{2,1,0:T(8,128)(4,1)S(1)} %get-tuple-element.310, pred[64,12,128]{2,1,0:T(8,128)(4,1)S(1)} %get-tuple-element.311, ...), kind=kLoop, calls=%fused_computation.1.clone.1 | loop fusion | flops 15925248 | bytes 10939392 | tf_op jit(solution)/shard_map/while/body/eval_jaxpr/jit(_where)/select_n | solution.py:21
  52.1 4.6 %fusion.46 = f32[1728,128]{1,0:T(8,128)S(1)} fusion(bf16[1536,128]{1,0:T(8,128)(2,1)S(1)} %bitcast.66, bf16[216,8,12,128]{3,2,1,0:T(8,128)(2,1)} %bitcast.64), kind=kOutput, calls=%fused_computation.5.clone.1 | convolution fusion | flops 679477248 | bytes 6586368 | tf_op jit(solution)/shard_map/while/body/eval_jaxpr/dot_general | solution.py:51
  56.7 1.6 fusion.45
  59.8 1.4 broadcast_compare_fusion.4
  61.2 6.0 %select_select_fusion.3 = (bf16[27,64,12,128]{3,2,1,0:T(8,128)(2,1)}, bf16[27,64,12,128]{3,2,1,0:T(8,128)(2,1)S(1)}) fusion(pred[64,12,128]{2,1,0:T(8,128)(4,1)S(1)} %get-tuple-element.309, pred[64,12,128]{2,1,0:T(8,128)(4,1)S(1)} %get-tuple-element.310, pred[64,12,128]{2,1,0:T(8,128)(4,1)S(1)} %get-tuple-element.311, ...), kind=kLoop, calls=%fused_computation.1.clone.1 | loop fusion | flops 15925248 | bytes 10939392 | tf_op jit(solution)/shard_map/while/body/eval_jaxpr/jit(_where)/select_n | solution.py:21
  67.2 1.0 constant_dynamic-slice_fusion.3
  68.2 4.6 %fusion.46 = f32[1728,128]{1,0:T(8,128)S(1)} fusion(bf16[1536,128]{1,0:T(8,128)(2,1)S(1)} %bitcast.66, bf16[216,8,12,128]{3,2,1,0:T(8,128)(2,1)} %bitcast.64), kind=kOutput, calls=%fused_computation.5.clone.1 | convolution fusion | flops 679477248 | bytes 6586368 | tf_op jit(solution)/shard_map/while/body/eval_jaxpr/dot_general | solution.py:51
  72.8 1.6 fusion.45
  75.7 2.6 %copy.26 = f32[1,2,27,64,64]{4,1,2,0,3:T(2,128)} copy(f32[1,2,27,64,64]{4,3,2,1,0:T(8,128)S(1)} %bitcast.68) | data formatting | bytes 1769472 | tf_op jit(solution)/shard_map/mul | solution.py:80
  79.5 98.4 %all-reduce.3.cloned.1.call-done = f32[1,2,27,64,64]{4,1,2,0,3:T(2,128)} async-done(((f32[1,2,27,64,64]{4,1,2,0,3:T(2,128)}), f32[1,2,27,64,64]{4,1,2,0,3:T(2,128)}) %all-reduce.3.cloned.1.call-update) | async-done | bytes 884752
  178.9 5.4 %all_gather.3 = f32[2,2,27,4,64]{4,3,2,1,0:T(4,128)S(1)} all-gather(f32[1,2,27,4,64]{4,3,2,1,0:T(4,128)S(1)} %copy.32), channel_id=1, replica_groups=mesh['space'=16,'tm'=2] {'tm'}, dimensions={0}, use_global_device_ids=true | all-gather | bytes 165888 | tf_op jit(solution)/shard_map/all_gather | solution.py:82
  186.0 30.0 %psum.7 = f32[8,2,27]{2,0,1:T(8,128)S(1)} all-reduce(f32[8,2,27]{2,0,1:T(8,128)S(1)} %pad_maximum_fusion), channel_id=1, replica_groups=mesh['space'=16,'tm'=2] {'space'}, use_global_device_ids=true, to_apply=%region_5.6 | all-reduce | flops 432 | bytes 3456 | tf_op jit(solution)/shard_map/psum | solution.py:84
  (54 shorter events, 12.0 us)
Async XLA Ops:
  7.2 3.8 %copy-start.1 = (s32[27,3]{0,1:T(4,128)S(1)}, s32[27,3]{0,1:T(4,128)}, u32[]{:S(2)}) copy-start(s32[27,3]{0,1:T(4,128)} %param.8) | copy-start | bytes 976
  7.2 170.8 %all-reduce.3.cloned.1.call-start = ((), (), s32[]{:S(2)}) async-start(), calls=%async_computation | async-start | bytes 3538944
  75.6 2.6 %copy-start.3 = (u32[32]{0:T(128)S(1)}, u32[32]{0:T(128)}, u32[]{:S(2)}) copy-start(u32[32]{0:T(128)} %constant.167) | copy-start | bytes 388
  75.7 3.9 %copy-start.2 = (s32[8,2]{0,1:T(2,128)S(1)}, s32[8,2]{0,1:T(2,128)}, u32[]{:S(2)}) copy-start(s32[8,2]{0,1:T(2,128)} %param.9) | copy-start | bytes 196
  178.9 7.0 %copy-start = (f32[1,2,27,4,64]{4,3,2,1,0:T(4,128)}, f32[1,2,27,4,64]{4,3,2,1,0:T(4,128)S(1)}, u32[]{:S(2)}) copy-start(f32[1,2,27,4,64]{4,3,2,1,0:T(4,128)S(1)} %copy.32) | copy-start | bytes 165892
Sparse Core Ops, SparseCore 0:
  78.4 99.5 all-reduce.2
where the time goes:
time: 224 us; the launch traced here: 223 us
  waiting for transfers between devices  98.4 us (44%)
  other arithmetic  35.8 us (16%)
  blocking collectives  35.4 us (16%)
  matrix products  25.9 us (12%)
  between operations  14.8 us (7%)
  local copies, waits for them, and re-layouts  12.7 us (6%)
    unnamed x2, waiting for transfers between devices  98.4 us
    psum x1, blocking collectives, local(): correlators = lax.psum(partial_traces, 'space') / nvec  30 us
    select_n x4, other arithmetic, phase_weights(): jnp.where(turns == 0, base_re, jnp.where(turns == 1, base_im, jnp.where(t...  23.8 us
    dot_general x4, matrix products, one_block(): left = jnp.dot(weight_re, stacked, preferred_element_type=jnp.float32)  18.3 us
    dot_general x4, matrix products, one_block(): right = jnp.dot(weight_im, stacked, preferred_element_type=jnp.float32)  6.29 us
    unnamed x13, local copies, waits for them, and re-layouts  5.89 us
    eq x4, other arithmetic, phase_weights(): turns == 0  5.79 us
    all_gather x1, blocking collectives, local(): every_slice = lax.all_gather(mesons, 'tm', axis=0, tiled=True)  5.42 us
  transfers between devices with their start and end apart: 1, of which 1 were waited for; matrix products, arithmetic and copies ran while one was open for 0% of the time, Pallas kernels for 0%

commit v1 on v0

--- a/solution.py
+++ b/solution.py
@@ -81,7 +81,7 @@
     mesons = lax.psum_scatter(terms, "space", scatter_dimension=3, tiled=True)
     every_slice = lax.all_gather(mesons, "tm", axis=0, tiled=True)
     partial_traces = pair_traces(every_slice, pairs)
-    correlators = lax.psum(partial_traces, "space") / nvec
+    correlators = jnp.sum(lax.all_gather(partial_traces, "space"), axis=0) / nvec
     return (mesons, correlators)
 
 

time: 224 us -> 214 us (0.955)
  blocking collectives: 35.4 us -> 24.9 us
    psum x1 -> x0, blocking collectives: 30 us -> none  [local(): correlators = lax.psum(partial_traces, 'space') / nvec]
    all_gather x0 -> x1, blocking collectives: none -> 19.5 us  [local(): lax.all_gather(partial_traces, 'space')]
where the time goes in v1:
time: 214 us; the launch traced here: 213 us
  waiting for transfers between devices  98.4 us (46%)
  other arithmetic  35.9 us (17%)
  matrix products  25.9 us (12%)
  blocking collectives  24.9 us (12%)
  between operations  14.8 us (7%)
  local copies, waits for them, and re-layouts  12.7 us (6%)
    unnamed x2, waiting for transfers between devices  98.4 us
    select_n x4, other arithmetic, phase_weights(): jnp.where(turns == 0, base_re, jnp.where(turns == 1, base_im, jnp.where(t...  23.8 us
    all_gather x1, blocking collectives, local(): lax.all_gather(partial_traces, 'space')  19.5 us
    dot_general x4, matrix products, one_block(): left = jnp.dot(weight_re, stacked, preferred_element_type=jnp.float32)  18.3 us
    dot_general x4, matrix products, one_block(): right = jnp.dot(weight_im, stacked, preferred_element_type=jnp.float32)  6.29 us
    unnamed x13, local copies, waits for them, and re-layouts  5.9 us
    eq x4, other arithmetic, phase_weights(): turns == 0  5.79 us
    all_gather x1, blocking collectives, local(): every_slice = lax.all_gather(mesons, 'tm', axis=0, tiled=True)  5.42 us
  transfers between devices with their start and end apart: 1, of which 1 were waited for; matrix products, arithmetic and copies ran while one was open for 0% of the time, Pallas kernels for 0%

profile of v1, /device:TPU:0, one launch (start us, length us, event | category | flops | bytes accessed | tf_op | source)
XLA Modules:
  0.0 213.0 jit_solution(9950295105683001082)
XLA Ops:
  7.2 3.7 %copy.66 = s32[1,64,12,512]{3,2,1,0:T(8,128)} copy(s32[1,64,12,512]{3,1,2,0:T(8,128)} %param.7) | data formatting | bytes 3145728 | tf_op args[1]
  11.0 64.5 %while.17 = (s32[]{:T(128)}, f32[2,1728,64]{2,1,0:T(8,128)S(1)}, s32[64,12,512]{2,1,0:T(8,128)}, s32[27,3]{0,1:T(4,128)S(1)}, s32[]{:T(128)}, /*index=5*/bf16[12...) while((s32[]{:T(128)}, f32[2,1728,64]{2,1,0:T(8,128)S(1)}, ...), condition=%wide.region_1.2_spmd.clone, body=%wide.region_0.1_spmd.clone.sunk | while | flops 1377275648 | bytes 30928840 | solution.py:58
  11.4 1.4 broadcast_compare_fusion.4
  12.8 6.0 %select_select_fusion.3 = (bf16[27,64,12,128]{3,2,1,0:T(8,128)(2,1)}, bf16[27,64,12,128]{3,2,1,0:T(8,128)(2,1)S(1)}) fusion(pred[64,12,128]{2,1,0:T(8,128)(4,1)S(1)} %get-tuple-element.311, pred[64,12,128]{2,1,0:T(8,128)(4,1)S(1)} %get-tuple-element.312, pred[64,12,128]{2,1,0:T(8,128)(4,1)S(1)} %get-tuple-element.313, ...), kind=kLoop, calls=%fused_computation.1.clone.1 | loop fusion | flops 15925248 | bytes 10939392 | tf_op jit(solution)/shard_map/while/body/eval_jaxpr/jit(_where)/select_n | solution.py:21
  18.8 1.0 constant_dynamic-slice_fusion.3
  19.8 4.6 %fusion.46 = f32[1728,128]{1,0:T(8,128)S(1)} fusion(bf16[1536,128]{1,0:T(8,128)(2,1)S(1)} %bitcast.69, bf16[216,8,12,128]{3,2,1,0:T(8,128)(2,1)} %bitcast.67), kind=kOutput, calls=%fused_computation.5.clone.1 | convolution fusion | flops 679477248 | bytes 6586368 | tf_op jit(solution)/shard_map/while/body/eval_jaxpr/dot_general | solution.py:51
  24.4 1.6 fusion.45
  27.5 1.4 broadcast_compare_fusion.4
  29.0 6.0 %select_select_fusion.3 = (bf16[27,64,12,128]{3,2,1,0:T(8,128)(2,1)}, bf16[27,64,12,128]{3,2,1,0:T(8,128)(2,1)S(1)}) fusion(pred[64,12,128]{2,1,0:T(8,128)(4,1)S(1)} %get-tuple-element.311, pred[64,12,128]{2,1,0:T(8,128)(4,1)S(1)} %get-tuple-element.312, pred[64,12,128]{2,1,0:T(8,128)(4,1)S(1)} %get-tuple-element.313, ...), kind=kLoop, calls=%fused_computation.1.clone.1 | loop fusion | flops 15925248 | bytes 10939392 | tf_op jit(solution)/shard_map/while/body/eval_jaxpr/jit(_where)/select_n | solution.py:21
  35.9 4.6 %fusion.46 = f32[1728,128]{1,0:T(8,128)S(1)} fusion(bf16[1536,128]{1,0:T(8,128)(2,1)S(1)} %bitcast.69, bf16[216,8,12,128]{3,2,1,0:T(8,128)(2,1)} %bitcast.67), kind=kOutput, calls=%fused_computation.5.clone.1 | convolution fusion | flops 679477248 | bytes 6586368 | tf_op jit(solution)/shard_map/while/body/eval_jaxpr/dot_general | solution.py:51
  40.5 1.6 fusion.45
  43.6 1.4 broadcast_compare_fusion.4
  45.1 6.0 %select_select_fusion.3 = (bf16[27,64,12,128]{3,2,1,0:T(8,128)(2,1)}, bf16[27,64,12,128]{3,2,1,0:T(8,128)(2,1)S(1)}) fusion(pred[64,12,128]{2,1,0:T(8,128)(4,1)S(1)} %get-tuple-element.311, pred[64,12,128]{2,1,0:T(8,128)(4,1)S(1)} %get-tuple-element.312, pred[64,12,128]{2,1,0:T(8,128)(4,1)S(1)} %get-tuple-element.313, ...), kind=kLoop, calls=%fused_computation.1.clone.1 | loop fusion | flops 15925248 | bytes 10939392 | tf_op jit(solution)/shard_map/while/body/eval_jaxpr/jit(_where)/select_n | solution.py:21
  52.1 4.6 %fusion.46 = f32[1728,128]{1,0:T(8,128)S(1)} fusion(bf16[1536,128]{1,0:T(8,128)(2,1)S(1)} %bitcast.69, bf16[216,8,12,128]{3,2,1,0:T(8,128)(2,1)} %bitcast.67), kind=kOutput, calls=%fused_computation.5.clone.1 | convolution fusion | flops 679477248 | bytes 6586368 | tf_op jit(solution)/shard_map/while/body/eval_jaxpr/dot_general | solution.py:51
  56.7 1.6 fusion.45
  59.8 1.4 broadcast_compare_fusion.4
  61.2 6.0 %select_select_fusion.3 = (bf16[27,64,12,128]{3,2,1,0:T(8,128)(2,1)}, bf16[27,64,12,128]{3,2,1,0:T(8,128)(2,1)S(1)}) fusion(pred[64,12,128]{2,1,0:T(8,128)(4,1)S(1)} %get-tuple-element.311, pred[64,12,128]{2,1,0:T(8,128)(4,1)S(1)} %get-tuple-element.312, pred[64,12,128]{2,1,0:T(8,128)(4,1)S(1)} %get-tuple-element.313, ...), kind=kLoop, calls=%fused_computation.1.clone.1 | loop fusion | flops 15925248 | bytes 10939392 | tf_op jit(solution)/shard_map/while/body/eval_jaxpr/jit(_where)/select_n | solution.py:21
  67.2 1.0 constant_dynamic-slice_fusion.3
  68.2 4.6 %fusion.46 = f32[1728,128]{1,0:T(8,128)S(1)} fusion(bf16[1536,128]{1,0:T(8,128)(2,1)S(1)} %bitcast.69, bf16[216,8,12,128]{3,2,1,0:T(8,128)(2,1)} %bitcast.67), kind=kOutput, calls=%fused_computation.5.clone.1 | convolution fusion | flops 679477248 | bytes 6586368 | tf_op jit(solution)/shard_map/while/body/eval_jaxpr/dot_general | solution.py:51
  72.8 1.6 fusion.45
  75.7 2.6 %copy.37 = f32[1,2,27,64,64]{4,1,2,0,3:T(2,128)} copy(f32[1,2,27,64,64]{4,3,2,1,0:T(8,128)S(1)} %bitcast.71) | data formatting | bytes 1769472 | tf_op jit(solution)/shard_map/mul | solution.py:80
  79.5 98.4 %all-reduce.3.cloned.1.call-done = f32[1,2,27,64,64]{4,1,2,0,3:T(2,128)} async-done(((f32[1,2,27,64,64]{4,1,2,0,3:T(2,128)}), f32[1,2,27,64,64]{4,1,2,0,3:T(2,128)}) %all-reduce.3.cloned.1.call-update) | async-done | bytes 884752
  178.9 5.4 %all_gather.9 = f32[2,2,27,4,64]{4,3,2,1,0:T(4,128)S(1)} all-gather(f32[1,2,27,4,64]{4,3,2,1,0:T(4,128)S(1)} %copy.43), channel_id=1, replica_groups=mesh['space'=16,'tm'=2] {'tm'}, dimensions={0}, use_global_device_ids=true | all-gather | bytes 165888 | tf_op jit(solution)/shard_map/all_gather | solution.py:82
  186.0 19.5 %all-gather = f32[128,2,27]{2,1,0:T(2,128)S(1)} all-gather(f32[8,2,27]{2,1,0:T(2,128)S(1)} %copy.41), channel_id=2, replica_groups=mesh['space'=16,'tm'=2] {'space'}, dimensions={0}, use_global_device_ids=true | all-gather | bytes 29376 | tf_op jit(solution)/shard_map/all_gather | solution.py:84
  (54 shorter events, 12.0 us)
Async XLA Ops:
  7.2 3.8 %copy-start.1 = (s32[27,3]{0,1:T(4,128)S(1)}, s32[27,3]{0,1:T(4,128)}, u32[]{:S(2)}) copy-start(s32[27,3]{0,1:T(4,128)} %param.8) | copy-start | bytes 976
  7.2 170.8 %all-reduce.3.cloned.1.call-start = ((), (), s32[]{:S(2)}) async-start(), calls=%async_computation | async-start | bytes 3538944
  75.6 2.6 %copy-start.3 = (u32[32]{0:T(128)S(1)}, u32[32]{0:T(128)}, u32[]{:S(2)}) copy-start(u32[32]{0:T(128)} %constant.167) | copy-start | bytes 388
  75.7 3.9 %copy-start.2 = (s32[8,2]{0,1:T(2,128)S(1)}, s32[8,2]{0,1:T(2,128)}, u32[]{:S(2)}) copy-start(s32[8,2]{0,1:T(2,128)} %param.9) | copy-start | bytes 196
  178.9 7.0 %copy-start = (f32[1,2,27,4,64]{4,3,2,1,0:T(4,128)}, f32[1,2,27,4,64]{4,3,2,1,0:T(4,128)S(1)}, u32[]{:S(2)}) copy-start(f32[1,2,27,4,64]{4,3,2,1,0:T(4,128)S(1)} %copy.43) | copy-start | bytes 165892
Sparse Core Ops, SparseCore 0:
  78.4 99.5 all-reduce.2
